TPU v7x, 32 devices: a whole 2x2x4 slice. The times are simulated.
32 devices in a mesh: rows: 32 (over z, y, x, core).
Axes of the slice: x: 2, y: 2, z: 4, core: 2. Of those that a mesh axis runs over, the one named last changes fastest.
Arguments:
- q_final: float32 [49152, 512], P('rows'), may hold values from -0.084712684 to 0.084712684
- r_first: float32 [512, 512], replicated, may hold values from -1 to 2, as said below
- r_second: float32 [512, 512], replicated, may hold values from -1 to 2, as said below
- q_grad: float32 [49152, 512], P('rows'), may hold values from -6 to 6
- r_grad: float32 [512, 512], replicated, may hold values from -1.5 to 1.5
Outputs:
- a_grad: float32 [49152, 512], P('rows')
Inputs may be any that keep to these rules, and one draw needn't show every extreme that they name: `r_first`: upper triangular, diagonal between 1 and 2. `r_second`: upper triangular, diagonal between 1 and 2.
All inputs are finite; a program needn't handle non-finite values.
Results may differ from a plain program's by a relative error of at most 0.000084.
Values sent between devices are 32-bit elements; how exact they have to be, the bound alone decides.
A program may use at most 128 MiB of HBM per device.

v0:
```python
import functools

import jax
import jax.numpy as jnp
from jax import lax
from jax.experimental import pallas as pl
from jax.experimental.pallas import tpu as pltpu
from jax.sharding import PartitionSpec as P

HIGH = lax.Precision.HIGH
MESH = pl.DeviceIdType.MESH
LANES = 128
FULL_ROWS = 96
VMEM_BYTES = 56 * 1024 * 1024


def iota2(shape):
    return lax.broadcasted_iota(jnp.int32, shape, 0), lax.broadcasted_iota(jnp.int32, shape, 1)


def split(x):
    high = x.astype(jnp.bfloat16)
    return high, (x - high.astype(jnp.float32)).astype(jnp.bfloat16)


def mm(a, b, dims=((1,), (0,))):
    a_high, a_low = split(a)
    b_high, b_low = split(b)
    dot = functools.partial(
        lax.dot_general, dimension_numbers=(dims, ((), ())), preferred_element_type=jnp.float32
    )
    return dot(a_high, b_high) + (dot(a_high, b_low) + dot(a_low, b_high))


NT = ((1,), (1,))


def base_inverses(blocks):
    order = blocks[0].shape[0]
    row, col = iota2((order, order))
    eye = row == col
    inverses = [jnp.where(eye, 1.0 / jnp.where(eye, block, 1.0), 0.0) for block in blocks]
    span = 1
    while span < order:
        mask = (row // (2 * span) == col // (2 * span)) & (row // span < col // span)
        right = [mm(jnp.where(mask, b, 0.0), i) for b, i in zip(blocks, inverses)]
        inverses = [i - mm(i, r) for i, r in zip(inverses, right)]
        span *= 2
    return inverses


def invert(uppers, outs):
    order = uppers[0].shape[0]
    base = LANES if order % LANES == 0 else order
    for out in outs:
        out[...] = jnp.zeros_like(out)
    spots = [(m, s) for m in range(len(uppers)) for s in range(0, order, base)]
    blocks = base_inverses([uppers[m][s : s + base, s : s + base] for m, s in spots])
    for (m, s), block in zip(spots, blocks):
        outs[m][s : s + base, s : s + base] = block
    span = base
    while span < order:
        work = []
        for m in range(len(uppers)):
            for s in range(0, order - span, 2 * span):
                e = min(s + 2 * span, order)
                right = mm(uppers[m][s : s + span, s + span : e], outs[m][s + span : e, s + span : e])
                work.append((m, s, e, right))
        for m, s, e, right in work:
            outs[m][s : s + span, s + span : e] = -mm(outs[m][s : s + span, s : s + span], right)
        span *= 2


def small_kernel(r1, r2, rg, inv1, inv2, v_out, h_out, e_out):
    invert((r1, r2), (inv1, inv2))
    v_out[...] = mm(inv1[...], inv2[...])
    w = mm(r1[...], rg[...], NT)
    h_out[...] = mm(r2[...], w)
    e_out[...] = mm(w, r2[...])


def plan(n, rows):
    bits = list(range(n.bit_length() - 1))
    rest = bits[1:]
    half = len(rest) // 2
    swapped = [rest[i ^ 1] if (i ^ 1) < len(rest) else rest[i] for i in range(len(rest))]
    orders = [rest, swapped, rest[half:] + rest[:half]]
    unit = rows // 8
    sizes = [3 * unit, 3 * unit, rows - 6 * unit]
    out, start = [], 0
    for order, size in zip(orders, sizes):
        out.append((start, size, bits[:1] + order))
        start += size
    return out


def reduce_kernel(n, p_ref, d_ref, out_ref, dout_ref, acc, recv, gat, dacc, drecv, send_sem, recv_sem, dsend, drecv_sem):
    me = lax.axis_index("rows")
    levels = n.bit_length() - 1
    order, width = p_ref.shape

    def partner(bit):
        step = 1 << bit
        return me + step * (1 - 2 * ((me // step) % 2))

    barrier = pltpu.get_barrier_semaphore()
    for bit in range(levels):
        pl.semaphore_signal(barrier, inc=1, device_id=(partner(bit),), device_id_type=MESH)
    pl.semaphore_wait(barrier, levels)

    for j in range(width // LANES):
        acc[j * order : (j + 1) * order, :] = p_ref[:, j * LANES : (j + 1) * LANES]
    dacc[0] = d_ref[...]

    streams = plan(n, acc.shape[0])
    state = [(start, size) for start, size, _ in streams]
    base = [0] * len(streams)
    slot0 = 0
    for i, (_, size, _) in enumerate(streams):
        base[i] = slot0
        slot0 += 2 * size
    trail = [[] for _ in streams]

    def at(ref, off, size):
        return ref.at[pl.ds(pl.multiple_of(off, 8), size), :]

    for k in range(levels):
        pending = []
        for i, (_, _, bits) in enumerate(streams):
            off, size = state[i]
            peer = partner(bits[k])
            mine = (me // (1 << bits[k])) % 2
            halve = (size // 2) % 8 == 0 and size > FULL_ROWS
            part = size // 2 if halve else size
            send_off = off + (1 - mine) * part if halve else off
            keep_off = off + mine * part if halve else off
            landing = recv.at[pl.ds(base[i], part), :]
            copy = pltpu.make_async_remote_copy(
                src_ref=at(acc, send_off, part), dst_ref=landing,
                send_sem=send_sem.at[i, k], recv_sem=recv_sem.at[i, k],
                device_id=(peer,), device_id_type=MESH,
            )
            copy.start()
            pending.append((i, copy, keep_off, part, landing))
            if halve:
                trail[i].append((peer, off, keep_off, part))
            base[i] += part
            state[i] = (keep_off, part)
        dcopy = pltpu.make_async_remote_copy(
            src_ref=dacc.at[k], dst_ref=drecv.at[k], send_sem=dsend.at[k], recv_sem=drecv_sem.at[k],
            device_id=(partner(k),), device_id_type=MESH,
        )
        dcopy.start()
        for i, copy, keep_off, part, landing in pending:
            copy.wait()
            target = acc if k < levels - 1 else gat
            rows = pl.ds(pl.multiple_of(keep_off, 8), part)
            target[rows, :] = acc[rows, :] + landing[...]
        dcopy.wait()
        dacc[k + 1] = dacc[k] + drecv[k]

    depth = max(len(t) for t in trail)
    for back in range(depth):
        pending = []
        for i in range(len(streams)):
            if back >= len(trail[i]):
                continue
            peer, _, keep_off, part = trail[i][len(trail[i]) - 1 - back]
            copy = pltpu.make_async_remote_copy(
                src_ref=at(gat, keep_off, part), dst_ref=at(gat, keep_off, part),
                send_sem=send_sem.at[i, levels + back], recv_sem=recv_sem.at[i, levels + back],
                device_id=(peer,), device_id_type=MESH,
            )
            copy.start()
            pending.append(copy)
        for copy in pending:
            copy.wait()

    for j in range(width // LANES):
        out_ref[:, j * LANES : (j + 1) * LANES] = gat[j * order : (j + 1) * order, :]
    dout_ref[...] = dacc[levels]


def all_sum(n, packed, diag):
    levels = n.bit_length() - 1
    if n != 1 << levels or n < 4:
        return lax.psum((packed, diag), "rows")
    rows = packed.size // LANES
    vmem = pl.BlockSpec(memory_space=pltpu.VMEM)
    return pl.pallas_call(
        functools.partial(reduce_kernel, n),
        out_shape=(
            jax.ShapeDtypeStruct(packed.shape, jnp.float32),
            jax.ShapeDtypeStruct(diag.shape, jnp.float32),
        ),
        in_specs=[vmem, vmem],
        out_specs=(vmem, vmem),
        scratch_shapes=[
            pltpu.VMEM((rows, LANES), jnp.float32),
            pltpu.VMEM((2 * rows, LANES), jnp.float32),
            pltpu.VMEM((rows, LANES), jnp.float32),
            pltpu.VMEM((levels + 1,) + diag.shape, jnp.float32),
            pltpu.VMEM((levels,) + diag.shape, jnp.float32),
            pltpu.SemaphoreType.DMA((3, 2 * levels)),
            pltpu.SemaphoreType.DMA((3, 2 * levels)),
            pltpu.SemaphoreType.DMA((levels,)),
            pltpu.SemaphoreType.DMA((levels,)),
        ],
        compiler_params=pltpu.CompilerParams(
            collective_id=0, has_side_effects=True, vmem_limit_bytes=VMEM_BYTES
        ),
        name="reduce",
    )(packed, diag)


def dot(a, b):
    return jnp.dot(a, b, precision=HIGH)


def dot_nt(a, b):
    return lax.dot_general(a, b, (((1,), (1,)), ((), ())), precision=HIGH)


def cross_product(left, right):
    return lax.dot_general(left, right, (((0,), (0,)), ((), ())), precision=HIGH)


def copy_lower(matrix):
    return jnp.tril(matrix) + jnp.tril(matrix, -1).T


def local(n, q_final, r_first, r_second, q_grad, r_grad):
    width = q_final.shape[1]
    row, col = iota2((width, width))
    lower = row >= col
    packed = jnp.where(lower, cross_product(q_grad, q_final), cross_product(q_final, q_final))
    diag = jnp.broadcast_to(jnp.sum(q_final * q_final, axis=0)[None, :], (8, width))
    vmem = pl.BlockSpec(memory_space=pltpu.VMEM)
    square = jax.ShapeDtypeStruct((width, width), jnp.float32)
    inv1, inv2, v, h, e = pl.pallas_call(
        small_kernel,
        out_shape=(square,) * 5,
        in_specs=[vmem] * 3,
        out_specs=(vmem,) * 5,
        compiler_params=pltpu.CompilerParams(vmem_limit_bytes=VMEM_BYTES),
        name="small",
    )(r_first, r_second, r_grad)
    packed, diag = all_sum(n, packed, diag)
    upper = jnp.where(row < col, packed, 0.0)
    gram = upper + upper.T + jnp.where(row == col, diag[0][None, :], 0.0)
    cross = jnp.where(lower, packed, 0.0)
    second_copy = copy_lower(h - cross)
    middle = jnp.tril(cross + dot(second_copy, gram))
    first_copy = copy_lower(e - dot(dot(inv2, middle), r_second))
    weight = dot_nt(second_copy, v) + dot_nt(dot(r_second, first_copy), inv1)
    return dot_nt(q_grad, v) + dot(q_final, weight)


def solution(mesh):
    n = mesh.shape["rows"]
    placed = (P("rows", None), P(), P(), P("rows", None), P())
    return jax.shard_map(
        functools.partial(local, n), mesh=mesh, in_specs=placed, out_specs=P("rows", None), check_vma=False
    )
```

profile of v0, /device:TPU:0, one launch (start us, length us, event | category | flops | bytes accessed | tf_op | source)
XLA Modules:
  0.0 109.2 jit_solution(117044742001108038)
XLA Ops:
  0.0 2.3 %multiply_reduce_fusion = f32[512]{0:T(512)S(1)} fusion(f32[1536,512]{1,0:T(8,128)} %param.5), kind=kLoop, calls=%fused_computation.2 | loop fusion | flops 1572352 | bytes 3147776 | tf_op jit(solution)/shard_map/reduce_sum | solution.py:237
  2.3 0.6 broadcast_in_dim.30.d_ref
  2.9 0.1 iota_compare_fusion.4
  3.0 0.3 copy.6
  3.4 0.4 copy-done.1
  3.8 2.8 %fusion.21 = f32[512,512]{1,0:T(8,128)S(1)} fusion(f32[1536,512]{1,0:T(8,128)S(1)} %copy-done, f32[1536,512]{1,0:T(8,128)S(1)} %copy-done.1), kind=kOutput, calls=%fused_computation.34 | convolution fusion | flops 2415919104 | bytes 7340032 | tf_op jit(solution)/shard_map/dot_general | solution.py:225
  6.6 3.8 %convolution_select_fusion.p_ref = f32[512,512]{1,0:T(8,128)} fusion(f32[512,512]{1,0:T(8,128)S(1)} %fusion.21, f32[1536,512]{1,0:T(8,128)S(1)} %copy-done.1), kind=kOutput, calls=%fused_computation.7 | convolution fusion | flops 2416443392 | bytes 5242880 | tf_op jit(solution)/shard_map/dot_general | solution.py:225
  10.4 35.6 %reduce.1 = (f32[512,512]{1,0:T(8,128)}, f32[8,512]{1,0:T(8,128)}) custom-call(f32[512,512]{1,0:T(8,128)} %convolution_select_fusion.p_ref, f32[8,512]{1,0:T(8,128)} %broadcast_in_dim.30.d_ref), custom_call_target="tpu_custom_call" | custom-call | tf_op jit(solution)/shard_map/reduce/pallas_call | solution.py:190
  46.0 0.7 slice.3
  46.7 2.5 %copy.7 = f32[512,512]{0,1:T(8,128)} copy(f32[512,512]{1,0:T(8,128)} %get-tuple-element.14) | data formatting | bytes 2097152 | tf_op jit(solution)/shard_map/reduce/pallas_call | solution.py:190
  49.2 2.3 %fusion.8 = f32[512,512]{1,0:T(8,128)} fusion(f32[512,512]{1,0:T(8,128)} %get-tuple-element.14), kind=kLoop, calls=%fused_computation.20 | loop fusion | flops 524288 | bytes 2097152 | tf_op jit(solution)/shard_map/jit(_where)/select_n | solution.py:249
  51.5 2.6 %copy.12 = f32[512,512]{0,1:T(8,128)} copy(f32[512,512]{1,0:T(8,128)} %fusion.8) | data formatting | bytes 2097152 | tf_op jit(solution)/shard_map/jit(_where)/select_n | solution.py:249
  54.1 10.8 %small.1 = (f32[512,512]{1,0:T(8,128)}, f32[512,512]{1,0:T(8,128)}, f32[512,512]{1,0:T(8,128)}, f32[512,512]{1,0:T(8,128)}, f32[512,512]{1,0:T(8,128)}) custom-call(f32[512,512]{1,0:T(8,128)} %r1.1, f32[512,512]{1,0:T(8,128)} %r2.1, f32[512,512]{1,0:T(8,128)} %rg.1), custom_call_target="tpu_custom_call" | custom-call | tf_op jit(solution)/shard_map/small/pallas_call | solution.py:240
  64.9 2.6 %copy.8 = f32[512,512]{0,1:T(8,128)} copy(f32[512,512]{1,0:T(8,128)} %get-tuple-element.13) | data formatting | bytes 2097152 | tf_op jit(solution)/shard_map/small/pallas_call | solution.py:240
  67.5 2.8 %fusion.14 = f32[512,512]{0,1:T(8,128)} fusion(f32[512,512]{0,1:T(8,128)} %copy.8, pred[512,512]{0,1:T(32,128)(4,1)S(1)} %copy.6, f32[512,512]{0,1:T(8,128)} %copy.7), kind=kLoop, calls=%fused_computation.27 | loop fusion | flops 524288 | bytes 3407872 | tf_op jit(solution)/shard_map/sub | solution.py:252
  70.3 2.5 %copy.9 = f32[512,512]{1,0:T(8,128)} copy(f32[512,512]{0,1:T(8,128)} %fusion.14) | data formatting | bytes 2097152 | tf_op jit(solution)/shard_map/sub | solution.py:252
  72.8 3.9 %fusion.1 = f32[512,512]{0,1:T(8,128)S(1)} fusion(pred[512,512]{0,1:T(32,128)(4,1)S(1)} %copy.6, f32[512,512]{0,1:T(8,128)} %copy.12, f32[512]{0:T(512)S(1)} %bitcast.31, f32[512,512]{0,1:T(8,128)} %copy.7, f32[512,512]{0,1:T(8,128)} %fusion.14, f32[512,512]{1,0:T(8,128)} %copy.9, s32[512]{0:T(512)S(1)} %iota_add_fusion, f32[512,512]{1,0:T(8,128)} %get-tuple-element.14), kind=kOutput, calls=%fused_computation.6 | convolution fusion | flops 808976384 | bytes 6557696 | tf_op jit(solution)/shard_map/dot_general | solution.py:217
  76.8 2.1 %fusion.15 = f32[512,512]{1,0:T(8,128)} fusion(f32[512,512]{1,0:T(8,128)S(1)} %copy-done.5, f32[512,512]{0,1:T(8,128)S(1)} %copy-done.3, f32[512,512]{1,0:T(8,128)S(1)} %copy-done.4, s32[512]{0:T(512)S(1)} %iota_add_fusion), kind=kOutput, calls=%fused_computation.28 | convolution fusion | flops 806617088 | bytes 4196352 | tf_op jit(solution)/shard_map/dot_general | solution.py:221
  78.8 0.0 copy-done.8
  78.8 2.0 %fusion.22 = f32[512,512]{1,0:T(8,128)} fusion(f32[512,512]{1,0:T(8,128)S(1)} %copy-done.8, f32[512,512]{0,1:T(8,128)S(1)} %fusion.1), kind=kOutput, calls=%fused_computation.35 | convolution fusion | flops 805306368 | bytes 3145728 | tf_op jit(solution)/shard_map/dot_general | solution.py:217
  80.9 2.5 %copy.14 = f32[512,512]{0,1:T(8,128)} copy(f32[512,512]{1,0:T(8,128)} %get-tuple-element.15) | data formatting | bytes 2097152 | tf_op jit(solution)/shard_map/small/pallas_call | solution.py:240
  83.4 3.8 %convolution_subtract_fusion = f32[512,512]{0,1:T(8,128)} fusion(f32[512,512]{0,1:T(8,128)} %copy.14, f32[512,512]{1,0:T(8,128)} %fusion.22, f32[512,512]{1,0:T(8,128)} %r2.1), kind=kOutput, calls=%fused_computation.4 | convolution fusion | flops 805568512 | bytes 4194304 | tf_op jit(solution)/shard_map/dot_general | solution.py:217
  87.2 2.6 %copy.16 = f32[512,512]{1,0:T(8,128)} copy(f32[512,512]{0,1:T(8,128)} %convolution_subtract_fusion) | data formatting | bytes 2097152 | tf_op jit(solution)/shard_map/sub | solution.py:254
  89.8 3.9 %fusion.2 = f32[512,512]{1,0:T(8,128)S(1)} fusion(f32[512,512]{1,0:T(8,128)} %r2.1, f32[512,512]{0,1:T(8,128)} %convolution_subtract_fusion, f32[512,512]{1,0:T(8,128)} %copy.16, s32[512]{0:T(512)S(1)} %iota_add_fusion), kind=kOutput, calls=%fused_computation.9 | convolution fusion | flops 806617088 | bytes 4196352 | tf_op jit(solution)/shard_map/dot_general | solution.py:217
  93.7 0.0 copy-done.7
  93.7 0.0 copy-done.9
  93.7 0.0 copy-start.6
  93.7 1.9 %convolution_add_fusion.1 = f32[512,512]{1,0:T(8,128)S(1)} fusion(f32[512,512]{1,0:T(8,128)S(1)} %copy-done.7, f32[512,512]{1,0:T(8,128)S(1)} %fusion.2, f32[512,512]{1,0:T(8,128)S(1)} %copy-done.9), kind=kOutput, calls=%fused_computation.3 | convolution fusion | flops 805568512 | bytes 4194304 | tf_op jit(solution)/shard_map/dot_general | solution.py:221
  95.6 0.0 copy-start.2
  95.6 3.1 %fusion.20 = f32[512,1536]{1,0:T(8,128)S(1)} fusion(f32[512,512]{1,0:T(8,128)S(1)} %copy-done.6, f32[1536,512]{1,0:T(8,128)S(1)} %copy-done), kind=kOutput, calls=%fused_computation.33 | convolution fusion | flops 2415919104 | bytes 7340032 | tf_op jit(solution)/shard_map/dot_general | solution.py:221
  98.7 7.0 %fusion = f32[1536,512]{0,1:T(8,128)} fusion(f32[512,1536]{1,0:T(8,128)S(1)} %fusion.20, f32[512,512]{1,0:T(8,128)S(1)} %convolution_add_fusion.1, f32[1536,512]{1,0:T(8,128)S(1)} %copy-done.2), kind=kOutput, calls=%fused_computation.1 | convolution fusion | flops 2416705536 | bytes 10485760 | tf_op jit(solution)/shard_map/dot_general | solution.py:217
  105.7 3.5 %copy.18 = f32[1536,512]{1,0:T(8,128)} copy(f32[1536,512]{0,1:T(8,128)} %fusion) | data formatting | bytes 6291456 | tf_op jit(solution)/shard_map/add | solution.py:256
  (15 shorter events, 0.0 us)
Async XLA Ops:
  0.0 3.4 %copy-start = (f32[1536,512]{1,0:T(8,128)S(1)}, f32[1536,512]{1,0:T(8,128)}, u32[]{:S(2)}) copy-start(f32[1536,512]{1,0:T(8,128)} %param.8) | copy-start | bytes 9437188
  0.0 3.8 %copy-start.1 = (f32[1536,512]{1,0:T(8,128)S(1)}, f32[1536,512]{1,0:T(8,128)}, u32[]{:S(2)}) copy-start(f32[1536,512]{1,0:T(8,128)} %param.5) | copy-start | bytes 9437188
  72.8 3.9 %copy-start.3 = (f32[512,512]{0,1:T(8,128)S(1)}, f32[512,512]{0,1:T(8,128)}, u32[]{:S(2)}) copy-start(f32[512,512]{0,1:T(8,128)} %fusion.14) | copy-start | bytes 3145732
  72.8 3.9 %copy-start.4 = (f32[512,512]{1,0:T(8,128)S(1)}, f32[512,512]{1,0:T(8,128)}, u32[]{:S(2)}) copy-start(f32[512,512]{1,0:T(8,128)} %copy.9) | copy-start | bytes 3145732
  72.8 3.9 %copy-start.5 = (f32[512,512]{1,0:T(8,128)S(1)}, f32[512,512]{1,0:T(8,128)}, u32[]{:S(2)}) copy-start(f32[512,512]{1,0:T(8,128)} %get-tuple-element.12) | copy-start | bytes 3145732
  76.7 2.1 %copy-start.8 = (f32[512,512]{1,0:T(8,128)S(1)}, f32[512,512]{1,0:T(8,128)}, u32[]{:S(2)}) copy-start(f32[512,512]{1,0:T(8,128)} %get-tuple-element.16) | copy-start | bytes 3145732
  89.8 3.9 %copy-start.7 = (f32[512,512]{1,0:T(8,128)S(1)}, f32[512,512]{1,0:T(8,128)}, u32[]{:S(2)}) copy-start(f32[512,512]{1,0:T(8,128)} %fusion.15) | copy-start | bytes 3145732
  89.8 3.9 %copy-start.9 = (f32[512,512]{1,0:T(8,128)S(1)}, f32[512,512]{1,0:T(8,128)}, u32[]{:S(2)}) copy-start(f32[512,512]{1,0:T(8,128)} %get-tuple-element.18) | copy-start | bytes 3145732
  93.7 1.9 %copy-start.6 = (f32[512,512]{1,0:T(8,128)S(1)}, f32[512,512]{1,0:T(8,128)}, u32[]{:S(2)}) copy-start(f32[512,512]{1,0:T(8,128)} %get-tuple-element.12) | copy-start | bytes 3145732
  95.6 3.1 %copy-start.2 = (f32[1536,512]{1,0:T(8,128)S(1)}, f32[1536,512]{1,0:T(8,128)}, u32[]{:S(2)}) copy-start(f32[1536,512]{1,0:T(8,128)} %param.5) | copy-start | bytes 9437188
where the time goes:
time: 110 us; the launch traced here: 109 us
  Pallas kernels  46.4 us (42%)
  matrix products  34.1 us (31%)
  local copies, waits for them, and re-layouts  21 us (19%)
  other arithmetic  7.53 us (7%)
    pallas_call x1, Pallas kernels, all_sum(): pl.pallas_call(functools.partial(reduce_kernel, n), out_shape=(jax.ShapeD...  35.6 us
    dot_general x5, matrix products, dot(): return jnp.dot(a, b, precision=HIGH)  20.6 us
    pallas_call x1, Pallas kernels, local(): pl.pallas_call(small_kernel, out_shape=(square,) * 5, in_specs=[vmem] * 3...  10.8 us
    dot_general x3, matrix products, dot_nt(): return lax.dot_general(a, b, (((1,), (1,)), ((), ())), precision=HIGH)  6.99 us
    dot_general x2, matrix products, cross_product(): lax.dot_general(left, right, (((0,), (0,)), ((), ())), precision=HIGH)  6.57 us
    pallas_call x2, local copies, waits for them, and re-layouts, local(): pl.pallas_call(small_kernel, out_shape=(square,) * 5, in_specs=[vmem] * 3...  5.09 us
    add x1, local copies, waits for them, and re-layouts, local(): return dot_nt(q_grad, v) + dot(q_final, weight)  3.54 us
    sub x1, other arithmetic, local(): second_copy = copy_lower(h - cross)  2.81 us

commit v1 on v0

--- a/solution.py
+++ b/solution.py
@@ -7,7 +7,6 @@
 from jax.experimental.pallas import tpu as pltpu
 from jax.sharding import PartitionSpec as P
 
-HIGH = lax.Precision.HIGH
 MESH = pl.DeviceIdType.MESH
 LANES = 128
 FULL_ROWS = 96
@@ -35,48 +34,124 @@
 NT = ((1,), (1,))
 
 
-def base_inverses(blocks):
-    order = blocks[0].shape[0]
-    row, col = iota2((order, order))
-    eye = row == col
-    inverses = [jnp.where(eye, 1.0 / jnp.where(eye, block, 1.0), 0.0) for block in blocks]
-    span = 1
-    while span < order:
-        mask = (row // (2 * span) == col // (2 * span)) & (row // span < col // span)
-        right = [mm(jnp.where(mask, b, 0.0), i) for b, i in zip(blocks, inverses)]
-        inverses = [i - mm(i, r) for i, r in zip(inverses, right)]
-        span *= 2
-    return inverses
-
-
-def invert(uppers, outs):
+TN = ((0,), (0,))
+
+
+def inverse_steps(uppers, outs):
     order = uppers[0].shape[0]
     base = LANES if order % LANES == 0 else order
-    for out in outs:
-        out[...] = jnp.zeros_like(out)
-    spots = [(m, s) for m in range(len(uppers)) for s in range(0, order, base)]
-    blocks = base_inverses([uppers[m][s : s + base, s : s + base] for m, s in spots])
-    for (m, s), block in zip(spots, blocks):
-        outs[m][s : s + base, s : s + base] = block
-    span = base
-    while span < order:
+    spots = [(m, slice(s, s + base)) for m in range(len(uppers)) for s in range(0, order, base)]
+
+    def init():
+        row, col = iota2((base, base))
+        eye = row == col
+        for out in outs:
+            out[...] = jnp.zeros_like(out)
+        for m, s in spots:
+            outs[m][s, s] = jnp.where(eye, 1.0 / jnp.where(eye, uppers[m][s, s], 1.0), 0.0)
+
+    def inner(span):
+        row, col = iota2((base, base))
+        mask = (row // (2 * span) == col // (2 * span)) & (row // span < col // span)
+        blocks = [outs[m][s, s] for m, s in spots]
+        right = [mm(jnp.where(mask, uppers[m][s, s], 0.0), i) for (m, s), i in zip(spots, blocks)]
+        for (m, s), i, r in zip(spots, blocks, right):
+            outs[m][s, s] = i - mm(i, r)
+
+    def corner(span):
         work = []
         for m in range(len(uppers)):
             for s in range(0, order - span, 2 * span):
-                e = min(s + 2 * span, order)
-                right = mm(uppers[m][s : s + span, s + span : e], outs[m][s + span : e, s + span : e])
-                work.append((m, s, e, right))
-        for m, s, e, right in work:
-            outs[m][s : s + span, s + span : e] = -mm(outs[m][s : s + span, s : s + span], right)
+                top, low = slice(s, s + span), slice(s + span, min(s + 2 * span, order))
+                work.append((m, top, low, mm(uppers[m][top, low], outs[m][low, low])))
+        for m, top, low, right in work:
+            outs[m][top, low] = -mm(outs[m][top, top], right)
+
+    steps, span = [init], 1
+    while span < order:
+        steps.append(functools.partial(inner if span < base else corner, span))
         span *= 2
-
-
-def small_kernel(r1, r2, rg, inv1, inv2, v_out, h_out, e_out):
-    invert((r1, r2), (inv1, inv2))
-    v_out[...] = mm(inv1[...], inv2[...])
-    w = mm(r1[...], rg[...], NT)
-    h_out[...] = mm(r2[...], w)
-    e_out[...] = mm(w, r2[...])
+    return steps
+
+
+def small_steps(r1, r2, rg, inv1, inv2, w, h, e, vh, vl):
+    def first():
+        w[...] = mm(r1[...], rg[...], NT)
+
+    def second():
+        h[...] = mm(r2[...], w[...])
+
+    def third():
+        e[...] = mm(w[...], r2[...])
+
+    def fourth():
+        vh[...], vl[...] = split(mm(inv1[...], inv2[...]).T)
+
+    return [first, second, third] + inverse_steps((r1, r2), (inv1, inv2)) + [fourth]
+
+
+def copy_lower(matrix):
+    row, col = iota2(matrix.shape)
+    return jnp.where(row >= col, matrix, 0.0) + jnp.where(row > col, matrix, 0.0).T
+
+
+def tail(packed, diag, r2, inv1, inv2, h, e, vh, vl, gram, second, third, bh, bl):
+    row, col = iota2(packed.shape)
+    upper = jnp.where(row < col, packed[...], 0.0)
+    gram[...] = upper + upper.T + jnp.where(row == col, diag[0:1, :], 0.0)
+    second[...] = copy_lower(h[...] - packed[...])
+    third[...] = packed[...] + mm(second[...], gram[...])
+    third[...] = mm(inv2[...], jnp.where(row >= col, third[...], 0.0))
+    third[...] = copy_lower(e[...] - mm(third[...], r2[...]))
+    third[...] = mm(r2[...], third[...])
+    third[...] = mm(third[...], inv1[...], NT)
+    s_high, s_low = split(second[...])
+    dot = functools.partial(jnp.dot, preferred_element_type=jnp.float32)
+    third[...] += dot(s_high, vh[...]) + (dot(s_high, vl[...]) + dot(s_low, vh[...]))
+    bh[...], bl[...] = split(third[...])
+
+
+def gram_kernel(q_ref, g_ref, out_ref, diag_ref, cross, gram):
+    step = pl.program_id(0)
+
+    @pl.when(step == 0)
+    def _():
+        cross[...] = jnp.zeros_like(cross)
+        gram[...] = jnp.zeros_like(gram)
+
+    half = q_ref.shape[1] // 2
+    low, top = slice(0, half), slice(half, 2 * half)
+    q1, q2, g1, g2 = q_ref[:, low], q_ref[:, top], g_ref[:, low], g_ref[:, top]
+    q1, q2, g1, g2 = split(q1), split(q2), split(g1), split(g2)
+
+    def product(a, b):
+        dot = functools.partial(
+            lax.dot_general, dimension_numbers=(TN, ((), ())), preferred_element_type=jnp.float32
+        )
+        return dot(a[0], b[0]) + (dot(a[0], b[1]) + dot(a[1], b[0]))
+
+    cross[low, low] += product(g1, q1)
+    cross[top, low] += product(g2, q1)
+    cross[top, top] += product(g2, q2)
+    gram[low, low] += product(q1, q1)
+    gram[low, top] += product(q1, q2)
+    gram[top, top] += product(q2, q2)
+
+    @pl.when(step == pl.num_programs(0) - 1)
+    def _():
+        row, col = iota2(out_ref.shape)
+        out_ref[...] = jnp.where(row >= col, cross[...], gram[...])
+        line = jnp.sum(jnp.where(row == col, gram[...], 0.0), axis=0, keepdims=True)
+        diag_ref[...] = jnp.broadcast_to(line, diag_ref.shape)
+
+
+def last_kernel(q_ref, g_ref, vh, vl, bh, bl, out_ref):
+    g_high, g_low = split(g_ref[...])
+    q_high, q_low = split(q_ref[...])
+    dot = functools.partial(jnp.dot, preferred_element_type=jnp.float32)
+    out_ref[...] = (dot(g_high, vh[...]) + dot(q_high, bh[...])) + (
+        (dot(g_high, vl[...]) + dot(g_low, vh[...])) + (dot(q_high, bl[...]) + dot(q_low, bh[...]))
+    )
 
 
 def plan(n, rows):
@@ -94,7 +169,11 @@
     return out
 
 
-def reduce_kernel(n, p_ref, d_ref, out_ref, dout_ref, acc, recv, gat, dacc, drecv, send_sem, recv_sem, dsend, drecv_sem):
+def reduce_kernel(
+    n, p_ref, d_ref, r1, r2, rg, vh, vl, bh, bl,
+    total, inv1, inv2, w, h, e, gram, second, third,
+    acc, recv, gat, dacc, drecv, send_sem, recv_sem, dsend, drecv_sem,
+):
     me = lax.axis_index("rows")
     levels = n.bit_length() - 1
     order, width = p_ref.shape
@@ -113,6 +192,12 @@
     dacc[0] = d_ref[...]
 
     streams = plan(n, acc.shape[0])
+    steps = small_steps(r1, r2, rg, inv1, inv2, w, h, e, vh, vl)
+
+    def fill(count):
+        for _ in range(min(count, len(steps))):
+            steps.pop(0)()
+
     state = [(start, size) for start, size, _ in streams]
     base = [0] * len(streams)
     slot0 = 0
@@ -151,6 +236,7 @@
             device_id=(partner(k),), device_id_type=MESH,
         )
         dcopy.start()
+        fill(2)
         for i, copy, keep_off, part, landing in pending:
             copy.wait()
             target = acc if k < levels - 1 else gat
@@ -173,29 +259,47 @@
             )
             copy.start()
             pending.append(copy)
+        fill(2)
         for copy in pending:
             copy.wait()
+    fill(len(steps))
 
     for j in range(width // LANES):
-        out_ref[:, j * LANES : (j + 1) * LANES] = gat[j * order : (j + 1) * order, :]
-    dout_ref[...] = dacc[levels]
-
-
-def all_sum(n, packed, diag):
+        total[:, j * LANES : (j + 1) * LANES] = gat[j * order : (j + 1) * order, :]
+    tail(total, dacc.at[levels], r2, inv1, inv2, h, e, vh, vl, gram, second, third, bh, bl)
+
+
+def alone_kernel(packed, diag, r1, r2, rg, vh, vl, bh, bl, inv1, inv2, w, h, e, gram, second, third):
+    for step in small_steps(r1, r2, rg, inv1, inv2, w, h, e, vh, vl):
+        step()
+    tail(packed, diag, r2, inv1, inv2, h, e, vh, vl, gram, second, third, bh, bl)
+
+
+def weights(n, packed, diag, r_first, r_second, r_grad):
     levels = n.bit_length() - 1
+    width = r_first.shape[0]
+    vmem = pl.BlockSpec(memory_space=pltpu.VMEM)
+    square = pltpu.VMEM((width, width), jnp.float32)
+    outs = (jax.ShapeDtypeStruct((width, width), jnp.bfloat16),) * 4
     if n != 1 << levels or n < 4:
-        return lax.psum((packed, diag), "rows")
+        packed, diag = lax.psum((packed, diag), "rows")
+        return pl.pallas_call(
+            alone_kernel,
+            out_shape=outs,
+            in_specs=[vmem] * 5,
+            out_specs=(vmem,) * 4,
+            scratch_shapes=[square] * 8,
+            compiler_params=pltpu.CompilerParams(vmem_limit_bytes=VMEM_BYTES),
+            name="weights",
+        )(packed, diag, r_first, r_second, r_grad)
     rows = packed.size // LANES
-    vmem = pl.BlockSpec(memory_space=pltpu.VMEM)
     return pl.pallas_call(
         functools.partial(reduce_kernel, n),
-        out_shape=(
-            jax.ShapeDtypeStruct(packed.shape, jnp.float32),
-            jax.ShapeDtypeStruct(diag.shape, jnp.float32),
-        ),
-        in_specs=[vmem, vmem],
-        out_specs=(vmem, vmem),
-        scratch_shapes=[
+        out_shape=outs,
+        in_specs=[vmem] * 5,
+        out_specs=(vmem,) * 4,
+        scratch_shapes=[square] * 9
+        + [
             pltpu.VMEM((rows, LANES), jnp.float32),
             pltpu.VMEM((2 * rows, LANES), jnp.float32),
             pltpu.VMEM((rows, LANES), jnp.float32),
@@ -209,51 +313,45 @@
         compiler_params=pltpu.CompilerParams(
             collective_id=0, has_side_effects=True, vmem_limit_bytes=VMEM_BYTES
         ),
-        name="reduce",
-    )(packed, diag)
-
-
-def dot(a, b):
-    return jnp.dot(a, b, precision=HIGH)
-
-
-def dot_nt(a, b):
-    return lax.dot_general(a, b, (((1,), (1,)), ((), ())), precision=HIGH)
-
-
-def cross_product(left, right):
-    return lax.dot_general(left, right, (((0,), (0,)), ((), ())), precision=HIGH)
-
-
-def copy_lower(matrix):
-    return jnp.tril(matrix) + jnp.tril(matrix, -1).T
+        name="weights",
+    )(packed, diag, r_first, r_second, r_grad)
+
+
+def tile_of(rows):
+    for tile in (512, 384, 256, 128, 64, 32, 16):
+        if rows % tile == 0:
+            return tile
+    return rows
 
 
 def local(n, q_final, r_first, r_second, q_grad, r_grad):
-    width = q_final.shape[1]
-    row, col = iota2((width, width))
-    lower = row >= col
-    packed = jnp.where(lower, cross_product(q_grad, q_final), cross_product(q_final, q_final))
-    diag = jnp.broadcast_to(jnp.sum(q_final * q_final, axis=0)[None, :], (8, width))
-    vmem = pl.BlockSpec(memory_space=pltpu.VMEM)
-    square = jax.ShapeDtypeStruct((width, width), jnp.float32)
-    inv1, inv2, v, h, e = pl.pallas_call(
-        small_kernel,
-        out_shape=(square,) * 5,
-        in_specs=[vmem] * 3,
-        out_specs=(vmem,) * 5,
+    rows, width = q_final.shape
+    tile = tile_of(rows)
+    rowspec = pl.BlockSpec((tile, width), lambda i: (i, 0))
+    fixed = pl.BlockSpec((width, width), lambda i: (0, 0))
+    packed, diag = pl.pallas_call(
+        gram_kernel,
+        grid=(rows // tile,),
+        out_shape=(
+            jax.ShapeDtypeStruct((width, width), jnp.float32),
+            jax.ShapeDtypeStruct((8, width), jnp.float32),
+        ),
+        in_specs=[rowspec, rowspec],
+        out_specs=(fixed, pl.BlockSpec((8, width), lambda i: (0, 0))),
+        scratch_shapes=[pltpu.VMEM((width, width), jnp.float32)] * 2,
         compiler_params=pltpu.CompilerParams(vmem_limit_bytes=VMEM_BYTES),
-        name="small",
-    )(r_first, r_second, r_grad)
-    packed, diag = all_sum(n, packed, diag)
-    upper = jnp.where(row < col, packed, 0.0)
-    gram = upper + upper.T + jnp.where(row == col, diag[0][None, :], 0.0)
-    cross = jnp.where(lower, packed, 0.0)
-    second_copy = copy_lower(h - cross)
-    middle = jnp.tril(cross + dot(second_copy, gram))
-    first_copy = copy_lower(e - dot(dot(inv2, middle), r_second))
-    weight = dot_nt(second_copy, v) + dot_nt(dot(r_second, first_copy), inv1)
-    return dot_nt(q_grad, v) + dot(q_final, weight)
+        name="grams",
+    )(q_final, q_grad)
+    split_weights = weights(n, packed, diag, r_first, r_second, r_grad)
+    return pl.pallas_call(
+        last_kernel,
+        grid=(rows // tile,),
+        out_shape=jax.ShapeDtypeStruct((rows, width), jnp.float32),
+        in_specs=[rowspec, rowspec] + [fixed] * 4,
+        out_specs=rowspec,
+        compiler_params=pltpu.CompilerParams(vmem_limit_bytes=VMEM_BYTES),
+        name="last",
+    )(q_final, q_grad, *split_weights)
 
 
 def solution(mesh):

time: 110 us -> 57.8 us (0.53)
  matrix products: 34.1 us -> 0 us
  local copies, waits for them, and re-layouts: 21 us -> 0 us
  Pallas kernels: 46.4 us -> 57.6 us
  other arithmetic: 7.53 us -> 0 us
    dot_general x10 -> x0, matrix products: 34.1 us -> none  [the longest x5 20.6 us: dot(): return jnp.dot(a, b, precision=HIGH)]
    pallas_call x2 -> x3, Pallas kernels: 46.4 us -> 57.6 us  [the longest x1 41.9 us: weights(): pl.pallas_call(functools.partial(reduce_kernel, n), out_shape=outs, in_sp...]
    pallas_call x3 -> x0, local copies, waits for them, and re-layouts: 7.61 us -> none  [the longest x2 5.09 us: local(): pl.pallas_call(small_kernel, out_shape=(square,) * 5, in_specs=[vmem] * 3...]
    sub x2 -> x0, local copies, waits for them, and re-layouts: 5.13 us -> none  [the longest x1 2.58 us: local(): first_copy = copy_lower(e - dot(dot(inv2, middle), r_second))]
    add x1 -> x0, local copies, waits for them, and re-layouts: 3.54 us -> none  [local(): return dot_nt(q_grad, v) + dot(q_final, weight)]
    sub x1 -> x0, other arithmetic: 2.81 us -> none  [local(): second_copy = copy_lower(h - cross)]
    select_n x1 -> x0, local copies, waits for them, and re-layouts: 2.56 us -> none  [local(): upper = jnp.where(row < col, packed, 0.0)]
    select_n x1 -> x0, other arithmetic: 2.32 us -> none  [local(): upper = jnp.where(row < col, packed, 0.0)]
where the time goes in v1:
time: 57.8 us; the launch traced here: 57.7 us
  Pallas kernels  57.6 us (100%)
    pallas_call x1, Pallas kernels, weights(): pl.pallas_call(functools.partial(reduce_kernel, n), out_shape=outs, in_sp...  41.9 us
    pallas_call x1, Pallas kernels, local(): pl.pallas_call(last_kernel, grid=(rows // tile,), out_shape=jax.ShapeDtyp...  8.65 us
    pallas_call x1, Pallas kernels, local(): pl.pallas_call(gram_kernel, grid=(rows // tile,), out_shape=(jax.ShapeDty...  7.12 us

profile of v1, /device:TPU:0, one launch (start us, length us, event | category | flops | bytes accessed | tf_op | source)
XLA Modules:
  0.0 57.7 jit_solution(8993884483424115615)
XLA Ops:
  0.0 7.1 %grams.1 = (f32[512,512]{1,0:T(8,128)}, f32[8,512]{1,0:T(8,128)}) custom-call(f32[1536,512]{1,0:T(8,128)} %q_ref.3, f32[1536,512]{1,0:T(8,128)} %g_ref.3), custom_call_target="tpu_custom_call" | custom-call | tf_op jit(solution)/shard_map/grams/pallas_call | solution.py:332
  7.1 41.9 %weights.1 = (bf16[512,512]{1,0:T(8,128)(2,1)}, bf16[512,512]{1,0:T(8,128)(2,1)}, bf16[512,512]{1,0:T(8,128)(2,1)}, bf16[512,512]{1,0:T(8,128)(2,1)}) custom-call(f32[512,512]{1,0:T(8,128)} %get-tuple-element.11.p_ref, f32[8,512]{1,0:T(8,128)} %get-tuple-element.12.d_ref, f32[512,512]{1,0:T(8,128)} %r1.1, f32[512,512]{1,0:T(8,128)} %r2.1, f32[512,512]{1,0:T(8,128)} %rg.1), custom_call_target="tpu_custom_call" | custom-call | tf_op jit(solution)/shard_map/weights/pallas_call | solution.py:296
  49.0 8.7 %last.1 = f32[1536,512]{1,0:T(8,128)} custom-call(f32[1536,512]{1,0:T(8,128)} %q_ref.3, f32[1536,512]{1,0:T(8,128)} %g_ref.3, bf16[512,512]{1,0:T(8,128)(2,1)} %get-tuple-element.13.vh, bf16[512,512]{1,0:T(8,128)(2,1)} %get-tuple-element.14.vl, bf16[512,512]{1,0:T(8,128)(2,1)} %get-tuple-element.15.bh, bf16[512,512]{1,0:T(8,128)(2,1)} %get-tuple-element.16.bl), custom_call_target="tpu_custom_call" | custom-call | tf_op jit(solution)/shard_map/last/pallas_call | solution.py:346

commit v2 on v1

--- a/solution.py
+++ b/solution.py
@@ -318,7 +318,7 @@
 
 
 def tile_of(rows):
-    for tile in (512, 384, 256, 128, 64, 32, 16):
+    for tile in (256, 128, 64, 32, 16):
         if rows % tile == 0:
             return tile
     return rows

time: 57.8 us -> 60.1 us (1.040)
  Pallas kernels: 57.6 us -> 59.7 us
    pallas_call x1, Pallas kernels: 7.12 us -> 8.3 us  [local(): pl.pallas_call(gram_kernel, grid=(rows // tile,), out_shape=(jax.ShapeDty...]
    pallas_call x1, Pallas kernels: 8.65 us -> 9.55 us  [local(): pl.pallas_call(last_kernel, grid=(rows // tile,), out_shape=jax.ShapeDtyp...]
where the time goes in v2:
time: 60.1 us; the launch traced here: 59.7 us
  Pallas kernels  59.7 us (99%)
    pallas_call x1, Pallas kernels, weights(): pl.pallas_call(functools.partial(reduce_kernel, n), out_shape=outs, in_sp...  41.9 us
    pallas_call x1, Pallas kernels, local(): pl.pallas_call(last_kernel, grid=(rows // tile,), out_shape=jax.ShapeDtyp...  9.55 us
    pallas_call x1, Pallas kernels, local(): pl.pallas_call(gram_kernel, grid=(rows // tile,), out_shape=(jax.ShapeDty...  8.3 us

profile of v2, /device:TPU:0, one launch (start us, length us, event | category | flops | bytes accessed | tf_op | source)
XLA Modules:
  0.0 59.7 jit_solution(9453456886631235477)
XLA Ops:
  0.0 8.3 %grams.1 = (f32[512,512]{1,0:T(8,128)}, f32[8,512]{1,0:T(8,128)}) custom-call(f32[1536,512]{1,0:T(8,128)} %q_ref.3, f32[1536,512]{1,0:T(8,128)} %g_ref.3), custom_call_target="tpu_custom_call" | custom-call | tf_op jit(solution)/shard_map/grams/pallas_call | solution.py:332
  8.3 41.9 %weights.1 = (bf16[512,512]{1,0:T(8,128)(2,1)}, bf16[512,512]{1,0:T(8,128)(2,1)}, bf16[512,512]{1,0:T(8,128)(2,1)}, bf16[512,512]{1,0:T(8,128)(2,1)}) custom-call(f32[512,512]{1,0:T(8,128)} %get-tuple-element.11.p_ref, f32[8,512]{1,0:T(8,128)} %get-tuple-element.12.d_ref, f32[512,512]{1,0:T(8,128)} %r1.1, f32[512,512]{1,0:T(8,128)} %r2.1, f32[512,512]{1,0:T(8,128)} %rg.1), custom_call_target="tpu_custom_call" | custom-call | tf_op jit(solution)/shard_map/weights/pallas_call | solution.py:296
  50.2 9.5 %last.1 = f32[1536,512]{1,0:T(8,128)} custom-call(f32[1536,512]{1,0:T(8,128)} %q_ref.3, f32[1536,512]{1,0:T(8,128)} %g_ref.3, bf16[512,512]{1,0:T(8,128)(2,1)} %get-tuple-element.13.vh, bf16[512,512]{1,0:T(8,128)(2,1)} %get-tuple-element.14.vl, bf16[512,512]{1,0:T(8,128)(2,1)} %get-tuple-element.15.bh, bf16[512,512]{1,0:T(8,128)(2,1)} %get-tuple-element.16.bl), custom_call_target="tpu_custom_call" | custom-call | tf_op jit(solution)/shard_map/last/pallas_call | solution.py:346
